TPU v7x, 32 devices: a whole 2x2x4 slice. The times are simulated.
32 devices in a mesh: section: 2 (over x), expert: 4 (over y, core), dp: 4 (over z).
Axes of the slice: x: 2, y: 2, z: 4, core: 2. Of those that a mesh axis runs over, the one named last changes fastest.
Arguments:
- x_in: bfloat16 [8, 256, 2048], P(None, ('expert', 'dp'), 'section'), may hold values from -6 to 6
- cotangent: bfloat16 [8, 256, 2048], P(None, ('expert', 'dp'), 'section'), may hold values from -6 to 6
- route_ids: int32 [2, 8, 256, 2], P('section', None, ('expert', 'dp')), may hold values from 0 to 15, all different within a row; in each aligned block of 16 rows (0 to 15, 16 to 31, ..., all dimensions but the last counted through in order) at most 2 rows name the same one
- norm_gain: float32 [2, 2048], P('section'), may hold values from 0.5 to 1.5
- router: bfloat16 [2, 2048, 16], P('section'), may hold values from -0.125 to 0.125
- w_gate_up: bfloat16 [2, 16, 2048, 1024], P('section', ('expert', 'dp')), may hold values from -0.125 to 0.125
- w_down: bfloat16 [2, 16, 512, 2048], P('section', ('expert', 'dp')), may hold values from -0.25 to 0.25
Outputs:
- grad_in: bfloat16 [8, 256, 2048], P(None, ('expert', 'dp'), 'section')
- grad_gate_up: float32 [2, 16, 2048, 1024], P('section', ('expert', 'dp'))
- grad_down: float32 [2, 16, 512, 2048], P('section', ('expert', 'dp'))
- grad_router: float32 [2, 2048, 16], P('section')
- grad_gain: float32 [2, 2048], P('section')
Inputs may be any that keep to these rules, and one draw needn't show every extreme that they name: `route_ids`: each row names two different experts; the 16 rows of one device in one layer and micro-batch name any expert at most 2 times, a bound that some block reaches in some of them.
All inputs are finite; a program needn't handle non-finite values.
Results may differ from a plain program's by a relative error of at most 0.035.
Values may be sent and summed in bfloat16 or wider, within the bound.
A program may use at most 64 MiB of HBM per device.

v0:
```python
import jax
import jax.numpy as jnp
from jax import lax
from jax.sharding import PartitionSpec as P

EPS = 1e-05


def shifted(value, axis, steps):
    count = lax.axis_size(axis)
    leading, last = (max(0, -steps), min(count, count - steps))
    return lax.ppermute(value, axis, [(source, source + steps) for source in range(leading, last)])


def keep_row(stash, position, value, active):
    old_row = lax.dynamic_index_in_dim(stash, position, 0, keepdims=False)
    return lax.dynamic_update_index_in_dim(stash, jnp.where(active, value, old_row), position, 0)


def slot_tables(route_rows, n_expert, capacity):
    experts = jnp.arange(n_expert, dtype=jnp.int32)
    expert_hits = (route_rows[:, :, None] == experts).astype(jnp.int32)
    per_expert = jnp.sum(expert_hits, axis=1)
    before = jnp.cumsum(per_expert, axis=0) - per_expert
    slot_ids = jnp.sum(expert_hits * before[:, None, :], axis=2)
    dest_cell = jnp.transpose(route_rows * capacity + slot_ids)
    cell_ids = jnp.arange(n_expert * capacity, dtype=jnp.int32)
    slot_place = (dest_cell[:, :, None] == cell_ids).astype(jnp.bfloat16)
    return (expert_hits.astype(jnp.float32), slot_place)


def norm_rows(layer_in, gain_vec):
    h_wide = layer_in.astype(jnp.float32)
    inv_rms = lax.rsqrt(jnp.mean(h_wide * h_wide, axis=-1, keepdims=True) + EPS)
    normed = (h_wide * inv_rms * gain_vec).astype(jnp.bfloat16)
    return (h_wide, inv_rms, normed)


def pair_gates(normed, router_mat, expert_hits):
    logits = jnp.dot(normed, router_mat, preferred_element_type=jnp.float32)
    chosen = jnp.sum(expert_hits * logits[:, None, :], axis=2)
    return (
        jax.nn.sigmoid(chosen[:, 0] - chosen[:, 1]),
        jax.nn.sigmoid(chosen[:, 1] - chosen[:, 0]),
    )


def expert_inner(exp_rows, w_gu):
    gate_up = jnp.einsum("sekd,edf->sekf", exp_rows, w_gu, preferred_element_type=jnp.float32)
    half_cols = w_gu.shape[2] // 2
    gate_part = gate_up[..., :half_cols]
    up_part = gate_up[..., half_cols:]
    sigmoid_gate = jax.nn.sigmoid(gate_part)
    hidden = (gate_part * sigmoid_gate * up_part).astype(jnp.bfloat16)
    return (gate_part, up_part, sigmoid_gate, hidden)


def expert_grads(gate_part, up_part, sigmoid_gate, dy_rows, w_gu, w_dn):
    d_hidden = jnp.einsum("sekd,efd->sekf", dy_rows, w_dn, preferred_element_type=jnp.float32)
    silu_gate = gate_part * sigmoid_gate
    silu_slope = sigmoid_gate * (1.0 + gate_part * (1.0 - sigmoid_gate))
    gate_up_grad = jnp.concatenate(
        [d_hidden * up_part * silu_slope, d_hidden * silu_gate], axis=-1
    ).astype(jnp.bfloat16)
    rows_grad = jnp.einsum(
        "sekf,edf->sekd", gate_up_grad, w_gu, preferred_element_type=jnp.float32
    ).astype(jnp.bfloat16)
    return (gate_up_grad, rows_grad)


def local(x_in, cotangent, route_ids, norm_gain, router, w_gate_up, w_down):
    micro_count, tok_rows, _ = x_in.shape
    n_segment = lax.axis_size("section")
    n_rank = lax.axis_size("expert") * lax.axis_size("dp")
    per_rank = w_down.shape[1]
    hidden_width = w_down.shape[2]
    model_width = w_down.shape[3]
    n_expert = per_rank * n_rank
    capacity = tok_rows * 2 * 9 // (8 * n_expert)
    cells = n_expert * capacity
    segment_idx = lax.axis_index("section")
    rows_shape = (n_rank, per_rank, capacity, model_width)
    x_all, top_all = (
        lax.all_gather(x_in, "section", axis=2, tiled=True),
        lax.all_gather(cotangent, "section", axis=2, tiled=True),
    )
    route_all = route_ids[0]
    gain_vec = norm_gain[0]
    router_mat = router[0]
    router_wide = router_mat.astype(jnp.float32)
    w_gu = w_gate_up[0]
    w_dn = w_down[0]
    ticks = micro_count + n_segment - 1

    def expert_forward(piece_rows):
        _, _, _, hidden = expert_inner(piece_rows, w_gu)
        out_rows = jnp.einsum(
            "sekf,efd->sekd", hidden, w_dn, preferred_element_type=jnp.float32
        ).astype(jnp.bfloat16)
        return (
            lax.all_to_all(out_rows, ("expert", "dp"), split_axis=0, concat_axis=0, tiled=True),
            piece_rows,
        )

    def forward_tick(tick_no, state_in):
        received, stash_h, stash_y, stash_x = state_in
        tick_slot = tick_no - segment_idx
        active = (tick_slot >= 0) & (tick_slot < micro_count)
        micro_idx = jnp.clip(tick_slot, 0, micro_count - 1)
        fresh_in = lax.dynamic_index_in_dim(x_all, micro_idx, 0, keepdims=False)
        layer_in = jnp.where(segment_idx == 0, fresh_in, received)
        h_wide, inv_rms, normed = norm_rows(layer_in, gain_vec)
        route_rows = lax.dynamic_index_in_dim(route_all, micro_idx, 0, keepdims=False)
        expert_hits, slot_place = slot_tables(route_rows, n_expert, capacity)
        send_rows = jnp.einsum("ktc,td->cd", slot_place, normed, preferred_element_type=jnp.float32)
        send_rows = send_rows.astype(jnp.bfloat16).reshape(rows_shape)
        returned, landed = expert_forward(
            lax.all_to_all(send_rows, ("expert", "dp"), split_axis=0, concat_axis=0, tiled=True)
        )
        back_flat = returned.reshape(cells, model_width)
        picked = jnp.einsum(
            "ktc,cd->ktd", slot_place, back_flat, preferred_element_type=jnp.float32
        )
        first_gate, second_gate = pair_gates(normed, router_mat, expert_hits)
        layer_out = (
            h_wide + first_gate[:, None] * picked[0] + second_gate[:, None] * picked[1]
        ).astype(jnp.bfloat16)
        passed = shifted(layer_out, "section", 1)
        stash_h = keep_row(stash_h, micro_idx, layer_in, active)
        stash_y = keep_row(stash_y, micro_idx, back_flat, active)
        stash_x = keep_row(stash_x, micro_idx, landed, active)
        return (passed, stash_h, stash_y, stash_x)

    start_fwd = (
        jnp.zeros((tok_rows, model_width), jnp.bfloat16),
        jnp.zeros((micro_count, tok_rows, model_width), jnp.bfloat16),
        jnp.zeros((micro_count, cells, model_width), jnp.bfloat16),
        jnp.zeros((micro_count,) + rows_shape, jnp.bfloat16),
    )
    _, stash_h, stash_y, stash_x = lax.fori_loop(0, ticks, forward_tick, start_fwd)

    def backward_tick(tick_no, state_in):
        received, keep_rows, keep_dy, keep_hidden, keep_dab, stash_grad, acc_router, acc_gain = (
            state_in
        )
        tick_slot = tick_no - (n_segment - 1 - segment_idx)
        active = (tick_slot >= 0) & (tick_slot < micro_count)
        micro_idx = jnp.clip(tick_slot, 0, micro_count - 1)
        fresh_top = lax.dynamic_index_in_dim(top_all, micro_idx, 0, keepdims=False)
        grad_top = jnp.where(segment_idx == n_segment - 1, fresh_top, received)
        grad_wide = grad_top.astype(jnp.float32)
        layer_in = lax.dynamic_index_in_dim(stash_h, micro_idx, 0, keepdims=False)
        h_wide, inv_rms, normed = norm_rows(layer_in, gain_vec)
        route_rows = lax.dynamic_index_in_dim(route_all, micro_idx, 0, keepdims=False)
        expert_hits, slot_place = slot_tables(route_rows, n_expert, capacity)
        first_gate, second_gate = pair_gates(normed, router_mat, expert_hits)
        gates = jnp.stack([first_gate, second_gate])
        scaled = (gates[:, :, None] * grad_wide[None]).astype(jnp.bfloat16)
        dy_send = jnp.einsum("ktc,ktd->cd", slot_place, scaled, preferred_element_type=jnp.float32)
        dy_send = dy_send.astype(jnp.bfloat16).reshape(rows_shape)
        exp_rows = lax.dynamic_index_in_dim(stash_x, micro_idx, 0, keepdims=False)
        dy_rows = lax.all_to_all(dy_send, ("expert", "dp"), split_axis=0, concat_axis=0, tiled=True)
        gate_part, up_part, sigmoid_gate, hidden = expert_inner(exp_rows, w_gu)
        gate_up_grad, rows_grad = expert_grads(
            gate_part, up_part, sigmoid_gate, dy_rows, w_gu, w_dn
        )
        back_grad = lax.all_to_all(
            rows_grad, ("expert", "dp"), split_axis=0, concat_axis=0, tiled=True
        )
        back_y = lax.dynamic_index_in_dim(stash_y, micro_idx, 0, keepdims=False)
        keep_dy = keep_row(keep_dy, micro_idx, dy_rows, active)
        keep_hidden = keep_row(keep_hidden, micro_idx, hidden, active)
        keep_dab = keep_row(keep_dab, micro_idx, gate_up_grad, active)
        normed_grad = jnp.einsum(
            "ktc,cd->td",
            slot_place,
            back_grad.reshape(cells, model_width),
            preferred_element_type=jnp.float32,
        )
        picked = jnp.einsum("ktc,cd->ktd", slot_place, back_y, preferred_element_type=jnp.float32)
        gate_grad = jnp.sum(grad_wide[None] * picked, axis=-1)
        logit_grad = first_gate * second_gate * (gate_grad[0] - gate_grad[1])
        logit_cols = logit_grad[:, None] * (expert_hits[:, 0, :] - expert_hits[:, 1, :])
        normed_grad = normed_grad + jnp.dot(
            logit_cols, router_wide.T, precision=lax.Precision.HIGHEST
        )
        router_term = jnp.dot(
            normed.astype(jnp.float32).T, logit_cols, precision=lax.Precision.HIGHEST
        )
        acc_router = acc_router + jnp.where(active, router_term, 0.0)
        acc_gain = acc_gain + jnp.where(
            active, jnp.sum(normed_grad * h_wide * inv_rms, axis=0), 0.0
        )
        scaled_grad = normed_grad * gain_vec
        projection = jnp.mean(scaled_grad * h_wide, axis=-1, keepdims=True)
        input_grad = (
            grad_wide + inv_rms * scaled_grad - h_wide * inv_rms * inv_rms * inv_rms * projection
        )
        grad_sent = input_grad.astype(jnp.bfloat16)
        stash_grad = keep_row(stash_grad, micro_idx, grad_sent, active)
        passed = shifted(grad_sent, "section", -1)
        return (passed, keep_rows, keep_dy, keep_hidden, keep_dab, stash_grad, acc_router, acc_gain)

    start_bwd = (
        jnp.zeros((tok_rows, model_width), jnp.bfloat16),
        stash_x,
        jnp.zeros((micro_count,) + rows_shape, jnp.bfloat16),
        jnp.zeros((micro_count, n_rank, per_rank, capacity, hidden_width), jnp.bfloat16),
        jnp.zeros((micro_count, n_rank, per_rank, capacity, 2 * hidden_width), jnp.bfloat16),
        jnp.zeros((micro_count, tok_rows, model_width), jnp.bfloat16),
        jnp.zeros((model_width, n_expert), jnp.float32),
        jnp.zeros((model_width,), jnp.float32),
    )
    final = lax.fori_loop(0, ticks, backward_tick, start_bwd)
    _, keep_rows, keep_dy, keep_hidden, keep_dab, stash_grad, acc_router, acc_gain = final
    grad_gu = jnp.einsum(
        "msekd,msekf->edf", keep_rows, keep_dab, preferred_element_type=jnp.float32
    )
    grad_dn = jnp.einsum(
        "msekf,msekd->efd", keep_hidden, keep_dy, preferred_element_type=jnp.float32
    )
    sum_router, sum_gain = (
        lax.psum(acc_router.astype(jnp.bfloat16), ("expert", "dp")).astype(jnp.float32),
        lax.psum(acc_gain.astype(jnp.bfloat16), ("expert", "dp")).astype(jnp.float32),
    )
    first_term = jnp.where(segment_idx == 0, stash_grad.astype(jnp.float32), 0.0)
    grad_in = lax.psum_scatter(
        first_term.astype(jnp.bfloat16), "section", scatter_dimension=2, tiled=True
    )
    return (grad_in, grad_gu[None], grad_dn[None], sum_router[None], sum_gain[None])


def solution(mesh):
    in_specs = (
        P(None, ("expert", "dp"), "section"),
        P(None, ("expert", "dp"), "section"),
        P("section", None, ("expert", "dp"), None),
        P("section", None),
        P("section", None, None),
        P("section", ("expert", "dp"), None, None),
        P("section", ("expert", "dp"), None, None),
    )
    out_specs = (
        P(None, ("expert", "dp"), "section"),
        P("section", ("expert", "dp"), None, None),
        P("section", ("expert", "dp"), None, None),
        P("section", None, None),
        P("section", None),
    )
    return jax.shard_map(local, mesh=mesh, in_specs=in_specs, out_specs=out_specs, check_vma=False)
```

profile of v0, /device:TPU:8, one launch (start us, length us, event | category | flops | bytes accessed | tf_op | source)
XLA Modules:
  0.0 864.4 jit_solution(11679668147466827216)
XLA Ops:
  8.1 10.6 %all_gather.6 = bf16[8,16,2048]{2,1,0:T(8,128)(2,1)} all-gather(bf16[8,16,1024]{2,1,0:T(8,128)(2,1)} %param.12), channel_id=1, replica_groups=mesh['section'=2,'expert'=4,'dp'=4] {'section'}, dimensions={2}, use_global_device_ids=true | all-gather | bytes 786432 | tf_op jit(solution)/shard_map/all_gather | solution.py:85
  18.6 8.9 %all_gather.7 = bf16[8,16,2048]{2,1,0:T(8,128)(2,1)} all-gather(bf16[8,16,1024]{2,1,0:T(8,128)(2,1)} %param.11), channel_id=1, replica_groups=mesh['section'=2,'expert'=4,'dp'=4] {'section'}, dimensions={2}, use_global_device_ids=true | all-gather | bytes 786432 | tf_op jit(solution)/shard_map/all_gather | solution.py:84
  31.9 327.4 %while.48 = (s32[]{:T(128)}, bf16[16,2048]{1,0:T(8,128)(2,1)S(1)}, bf16[8,16,2048]{2,1,0:T(8,128)(2,1)S(1)}, bf16[8,32,2048]{2,1,0:T(8,128)(2,1)}, bf16[8,16,1,2...) while((s32[]{:T(128)}, bf16[16,2048]{1,0:T(8,128)(2,1)S(1)}, ...), condition=%wide.region_7.8_spmd, body=%wide.region_0.7_spmd.sunk | while | flops 209598352 | bytes 11630114 | solution.py:140
  35.7 6.3 all-to-all-start
  52.2 4.8 all-to-all-start.1
  57.8 5.3 all-to-all-done.1
  72.5 4.8 all-to-all-start
  87.7 4.8 all-to-all-start.1
  93.3 5.3 all-to-all-done.1
  108.9 4.8 all-to-all-start
  124.0 4.8 all-to-all-start.1
  129.6 5.3 all-to-all-done.1
  145.2 4.8 all-to-all-start
  160.3 4.8 all-to-all-start.1
  165.9 5.3 all-to-all-done.1
  181.5 4.8 all-to-all-start
  196.6 4.8 all-to-all-start.1
  202.2 5.3 all-to-all-done.1
  217.8 4.8 all-to-all-start
  238.5 5.3 all-to-all-done.1
  254.1 4.8 all-to-all-start
  274.9 5.3 all-to-all-done.1
  290.5 4.8 all-to-all-start
  311.2 5.3 all-to-all-done.1
  326.8 4.8 all-to-all-start
  347.5 5.3 all-to-all-done.1
  363.5 403.9 %while.49 = (s32[]{:T(128)}, bf16[16,2048]{1,0:T(8,128)(2,1)S(1)}, bf16[8,16,1,2,2048]{4,3,1,2,0:T(2,128)(2,1)}, bf16[8,16,1,2,512]{4,1,3,2,0:T(8,128)(2,1)}, bf...) while((s32[]{:T(128)}, bf16[16,2048]{1,0:T(8,128)(2,1)S(1)}, ...), condition=%wide.region_18.19_spmd.clone, body=%wide.region_8.18_spmd.clone.sunk | while | flops 361911744 | bytes 17806364 | solution.py:214
  369.7 4.8 all-to-all-start.2
  387.4 6.1 all-to-all-start.3
  414.5 4.8 all-to-all-start.2
  432.2 6.1 all-to-all-start.3
  459.4 4.8 all-to-all-start.2
  477.1 6.1 all-to-all-start.3
  504.3 4.8 all-to-all-start.2
  522.0 6.1 all-to-all-start.3
  549.2 4.8 all-to-all-start.2
  566.9 6.1 all-to-all-start.3
  594.0 4.8 all-to-all-start.2
  611.7 6.1 all-to-all-start.3
  638.9 4.8 all-to-all-start.2
  656.6 6.1 all-to-all-start.3
  683.8 4.8 all-to-all-start.2
  701.5 6.1 all-to-all-start.3
  728.7 4.8 all-to-all-start.2
  746.4 6.1 all-to-all-start.3
  770.1 6.2 convolution_bitcast_fusion.1
  776.3 32.1 %psum.15 = bf16[1,2048]{1,0:T(2,128)(2,1)S(1)} all-reduce(bf16[1,2048]{1,0:T(2,128)(2,1)S(1)} %broadcast_in_dim.182), channel_id=1, replica_groups=mesh['section'=2,'expert'=4,'dp'=4] {'expert','dp'}, use_global_device_ids=true, to_apply=%region_21.22 | all-reduce | flops 2048 | bytes 8192 | tf_op jit(solution)/shard_map/psum | solution.py:224
  812.1 43.3 %all-reduce.2.cloned.1.call-done = bf16[1,2048,16]{1,2,0:T(8,128)(2,1)} async-done(((bf16[1,2048,16]{1,2,0:T(8,128)(2,1)}), bf16[1,2048,16]{1,2,0:T(8,128)(2,1)}) %all-reduce.2.cloned.1.call-update) | async-done | bytes 65552 | tf_op jit(solution)/shard_map/psum | solution.py:223
  (713 shorter events, 531.9 us)
Async XLA Ops:
  8.0 847.5 %all-reduce.2.cloned.1.call-start = ((), (), s32[]{:S(2)}) async-start(), calls=%async_computation.6 | async-start | bytes 131072 | tf_op jit(solution)/shard_map/psum | solution.py:223
  35.7 12.3 %all-to-all-start = ((bf16[16,1,2,2048]{3,2,1,0:T(2,128)(2,1)}), bf16[16,1,2,2048]{3,2,1,0:T(2,128)(2,1)S(1)}, u32[]{:S(2)}, u32[]{:S(2)}) async-start(bf16[16,1,2,2048]{3,2,1,0:T(2,128)(2,1)} %bitcast.324), calls=%async_computation | async-start | bytes 262144 | tf_op jit(solution)/shard_map/while/body/eval_jaxpr/all_to_all | solution.py:118
  52.2 10.9 %all-to-all-start.1 = ((bf16[16,1,2,2048]{3,2,1,0:T(2,128)(2,1)}), bf16[16,1,2,2048]{3,2,1,0:T(2,128)(2,1)S(1)}, u32[]{:S(2)}, u32[]{:S(2)}) async-start(bf16[16,1,2,2048]{3,2,1,0:T(2,128)(2,1)} %copy.84), calls=%async_computation.1 | async-start | bytes 262144 | tf_op jit(solution)/shard_map/while/body/eval_jaxpr/all_to_all | solution.py:101
  72.5 10.9 %all-to-all-start = ((bf16[16,1,2,2048]{3,2,1,0:T(2,128)(2,1)}), bf16[16,1,2,2048]{3,2,1,0:T(2,128)(2,1)S(1)}, u32[]{:S(2)}, u32[]{:S(2)}) async-start(bf16[16,1,2,2048]{3,2,1,0:T(2,128)(2,1)} %bitcast.324), calls=%async_computation | async-start | bytes 262144 | tf_op jit(solution)/shard_map/while/body/eval_jaxpr/all_to_all | solution.py:118
  87.7 10.9 %all-to-all-start.1 = ((bf16[16,1,2,2048]{3,2,1,0:T(2,128)(2,1)}), bf16[16,1,2,2048]{3,2,1,0:T(2,128)(2,1)S(1)}, u32[]{:S(2)}, u32[]{:S(2)}) async-start(bf16[16,1,2,2048]{3,2,1,0:T(2,128)(2,1)} %copy.84), calls=%async_computation.1 | async-start | bytes 262144 | tf_op jit(solution)/shard_map/while/body/eval_jaxpr/all_to_all | solution.py:101
  98.9 6.2 collective-permute-start
  108.9 10.9 %all-to-all-start = ((bf16[16,1,2,2048]{3,2,1,0:T(2,128)(2,1)}), bf16[16,1,2,2048]{3,2,1,0:T(2,128)(2,1)S(1)}, u32[]{:S(2)}, u32[]{:S(2)}) async-start(bf16[16,1,2,2048]{3,2,1,0:T(2,128)(2,1)} %bitcast.324), calls=%async_computation | async-start | bytes 262144 | tf_op jit(solution)/shard_map/while/body/eval_jaxpr/all_to_all | solution.py:118
  124.0 10.9 %all-to-all-start.1 = ((bf16[16,1,2,2048]{3,2,1,0:T(2,128)(2,1)}), bf16[16,1,2,2048]{3,2,1,0:T(2,128)(2,1)S(1)}, u32[]{:S(2)}, u32[]{:S(2)}) async-start(bf16[16,1,2,2048]{3,2,1,0:T(2,128)(2,1)} %copy.84), calls=%async_computation.1 | async-start | bytes 262144 | tf_op jit(solution)/shard_map/while/body/eval_jaxpr/all_to_all | solution.py:101
  135.2 6.2 collective-permute-start
  145.2 10.9 %all-to-all-start = ((bf16[16,1,2,2048]{3,2,1,0:T(2,128)(2,1)}), bf16[16,1,2,2048]{3,2,1,0:T(2,128)(2,1)S(1)}, u32[]{:S(2)}, u32[]{:S(2)}) async-start(bf16[16,1,2,2048]{3,2,1,0:T(2,128)(2,1)} %bitcast.324), calls=%async_computation | async-start | bytes 262144 | tf_op jit(solution)/shard_map/while/body/eval_jaxpr/all_to_all | solution.py:118
  160.3 10.9 %all-to-all-start.1 = ((bf16[16,1,2,2048]{3,2,1,0:T(2,128)(2,1)}), bf16[16,1,2,2048]{3,2,1,0:T(2,128)(2,1)S(1)}, u32[]{:S(2)}, u32[]{:S(2)}) async-start(bf16[16,1,2,2048]{3,2,1,0:T(2,128)(2,1)} %copy.84), calls=%async_computation.1 | async-start | bytes 262144 | tf_op jit(solution)/shard_map/while/body/eval_jaxpr/all_to_all | solution.py:101
  171.6 6.2 collective-permute-start
  181.5 10.9 %all-to-all-start = ((bf16[16,1,2,2048]{3,2,1,0:T(2,128)(2,1)}), bf16[16,1,2,2048]{3,2,1,0:T(2,128)(2,1)S(1)}, u32[]{:S(2)}, u32[]{:S(2)}) async-start(bf16[16,1,2,2048]{3,2,1,0:T(2,128)(2,1)} %bitcast.324), calls=%async_computation | async-start | bytes 262144 | tf_op jit(solution)/shard_map/while/body/eval_jaxpr/all_to_all | solution.py:118
  196.6 10.9 %all-to-all-start.1 = ((bf16[16,1,2,2048]{3,2,1,0:T(2,128)(2,1)}), bf16[16,1,2,2048]{3,2,1,0:T(2,128)(2,1)S(1)}, u32[]{:S(2)}, u32[]{:S(2)}) async-start(bf16[16,1,2,2048]{3,2,1,0:T(2,128)(2,1)} %copy.84), calls=%async_computation.1 | async-start | bytes 262144 | tf_op jit(solution)/shard_map/while/body/eval_jaxpr/all_to_all | solution.py:101
  207.9 6.2 collective-permute-start
  217.8 10.9 %all-to-all-start = ((bf16[16,1,2,2048]{3,2,1,0:T(2,128)(2,1)}), bf16[16,1,2,2048]{3,2,1,0:T(2,128)(2,1)S(1)}, u32[]{:S(2)}, u32[]{:S(2)}) async-start(bf16[16,1,2,2048]{3,2,1,0:T(2,128)(2,1)} %bitcast.324), calls=%async_computation | async-start | bytes 262144 | tf_op jit(solution)/shard_map/while/body/eval_jaxpr/all_to_all | solution.py:118
  233.0 10.9 %all-to-all-start.1 = ((bf16[16,1,2,2048]{3,2,1,0:T(2,128)(2,1)}), bf16[16,1,2,2048]{3,2,1,0:T(2,128)(2,1)S(1)}, u32[]{:S(2)}, u32[]{:S(2)}) async-start(bf16[16,1,2,2048]{3,2,1,0:T(2,128)(2,1)} %copy.84), calls=%async_computation.1 | async-start | bytes 262144 | tf_op jit(solution)/shard_map/while/body/eval_jaxpr/all_to_all | solution.py:101
  244.2 6.2 collective-permute-start
  254.1 10.9 %all-to-all-start = ((bf16[16,1,2,2048]{3,2,1,0:T(2,128)(2,1)}), bf16[16,1,2,2048]{3,2,1,0:T(2,128)(2,1)S(1)}, u32[]{:S(2)}, u32[]{:S(2)}) async-start(bf16[16,1,2,2048]{3,2,1,0:T(2,128)(2,1)} %bitcast.324), calls=%async_computation | async-start | bytes 262144 | tf_op jit(solution)/shard_map/while/body/eval_jaxpr/all_to_all | solution.py:118
  269.3 10.9 %all-to-all-start.1 = ((bf16[16,1,2,2048]{3,2,1,0:T(2,128)(2,1)}), bf16[16,1,2,2048]{3,2,1,0:T(2,128)(2,1)S(1)}, u32[]{:S(2)}, u32[]{:S(2)}) async-start(bf16[16,1,2,2048]{3,2,1,0:T(2,128)(2,1)} %copy.84), calls=%async_computation.1 | async-start | bytes 262144 | tf_op jit(solution)/shard_map/while/body/eval_jaxpr/all_to_all | solution.py:101
  280.5 6.2 collective-permute-start
  290.5 10.9 %all-to-all-start = ((bf16[16,1,2,2048]{3,2,1,0:T(2,128)(2,1)}), bf16[16,1,2,2048]{3,2,1,0:T(2,128)(2,1)S(1)}, u32[]{:S(2)}, u32[]{:S(2)}) async-start(bf16[16,1,2,2048]{3,2,1,0:T(2,128)(2,1)} %bitcast.324), calls=%async_computation | async-start | bytes 262144 | tf_op jit(solution)/shard_map/while/body/eval_jaxpr/all_to_all | solution.py:118
  305.6 10.9 %all-to-all-start.1 = ((bf16[16,1,2,2048]{3,2,1,0:T(2,128)(2,1)}), bf16[16,1,2,2048]{3,2,1,0:T(2,128)(2,1)S(1)}, u32[]{:S(2)}, u32[]{:S(2)}) async-start(bf16[16,1,2,2048]{3,2,1,0:T(2,128)(2,1)} %copy.84), calls=%async_computation.1 | async-start | bytes 262144 | tf_op jit(solution)/shard_map/while/body/eval_jaxpr/all_to_all | solution.py:101
  316.8 6.2 collective-permute-start
  326.8 10.9 %all-to-all-start = ((bf16[16,1,2,2048]{3,2,1,0:T(2,128)(2,1)}), bf16[16,1,2,2048]{3,2,1,0:T(2,128)(2,1)S(1)}, u32[]{:S(2)}, u32[]{:S(2)}) async-start(bf16[16,1,2,2048]{3,2,1,0:T(2,128)(2,1)} %bitcast.324), calls=%async_computation | async-start | bytes 262144 | tf_op jit(solution)/shard_map/while/body/eval_jaxpr/all_to_all | solution.py:118
  341.9 10.9 %all-to-all-start.1 = ((bf16[16,1,2,2048]{3,2,1,0:T(2,128)(2,1)}), bf16[16,1,2,2048]{3,2,1,0:T(2,128)(2,1)S(1)}, u32[]{:S(2)}, u32[]{:S(2)}) async-start(bf16[16,1,2,2048]{3,2,1,0:T(2,128)(2,1)} %copy.84), calls=%async_computation.1 | async-start | bytes 262144 | tf_op jit(solution)/shard_map/while/body/eval_jaxpr/all_to_all | solution.py:101
  353.2 6.2 collective-permute-start
  369.7 12.5 %all-to-all-start.2 = ((bf16[16,1,2,2048]{3,2,1,0:T(2,128)(2,1)}), bf16[16,1,2,2048]{3,2,1,0:T(2,128)(2,1)S(1)}, u32[]{:S(2)}, u32[]{:S(2)}) async-start(bf16[16,1,2,2048]{3,2,1,0:T(2,128)(2,1)} %bitcast.359), calls=%async_computation.2 | async-start | bytes 262144 | tf_op jit(solution)/shard_map/while/body/eval_jaxpr/all_to_all | solution.py:162
  387.4 12.0 %all-to-all-start.3 = ((bf16[16,1,2,2048]{3,2,1,0:T(2,128)(2,1)}), bf16[16,1,2,2048]{3,2,1,0:T(2,128)(2,1)S(1)}, u32[]{:S(2)}, u32[]{:S(2)}) async-start(bf16[16,1,2,2048]{3,2,1,0:T(2,128)(2,1)} %copy.87), calls=%async_computation.3 | async-start | bytes 262144 | tf_op jit(solution)/shard_map/while/body/eval_jaxpr/all_to_all | solution.py:167
  402.2 6.1 collective-permute-start.1
  414.5 12.6 %all-to-all-start.2 = ((bf16[16,1,2,2048]{3,2,1,0:T(2,128)(2,1)}), bf16[16,1,2,2048]{3,2,1,0:T(2,128)(2,1)S(1)}, u32[]{:S(2)}, u32[]{:S(2)}) async-start(bf16[16,1,2,2048]{3,2,1,0:T(2,128)(2,1)} %bitcast.359), calls=%async_computation.2 | async-start | bytes 262144 | tf_op jit(solution)/shard_map/while/body/eval_jaxpr/all_to_all | solution.py:162
  432.2 12.0 %all-to-all-start.3 = ((bf16[16,1,2,2048]{3,2,1,0:T(2,128)(2,1)}), bf16[16,1,2,2048]{3,2,1,0:T(2,128)(2,1)S(1)}, u32[]{:S(2)}, u32[]{:S(2)}) async-start(bf16[16,1,2,2048]{3,2,1,0:T(2,128)(2,1)} %copy.87), calls=%async_computation.3 | async-start | bytes 262144 | tf_op jit(solution)/shard_map/while/body/eval_jaxpr/all_to_all | solution.py:167
  459.4 12.6 %all-to-all-start.2 = ((bf16[16,1,2,2048]{3,2,1,0:T(2,128)(2,1)}), bf16[16,1,2,2048]{3,2,1,0:T(2,128)(2,1)S(1)}, u32[]{:S(2)}, u32[]{:S(2)}) async-start(bf16[16,1,2,2048]{3,2,1,0:T(2,128)(2,1)} %bitcast.359), calls=%async_computation.2 | async-start | bytes 262144 | tf_op jit(solution)/shard_map/while/body/eval_jaxpr/all_to_all | solution.py:162
  477.1 12.0 %all-to-all-start.3 = ((bf16[16,1,2,2048]{3,2,1,0:T(2,128)(2,1)}), bf16[16,1,2,2048]{3,2,1,0:T(2,128)(2,1)S(1)}, u32[]{:S(2)}, u32[]{:S(2)}) async-start(bf16[16,1,2,2048]{3,2,1,0:T(2,128)(2,1)} %copy.87), calls=%async_computation.3 | async-start | bytes 262144 | tf_op jit(solution)/shard_map/while/body/eval_jaxpr/all_to_all | solution.py:167
  504.3 12.6 %all-to-all-start.2 = ((bf16[16,1,2,2048]{3,2,1,0:T(2,128)(2,1)}), bf16[16,1,2,2048]{3,2,1,0:T(2,128)(2,1)S(1)}, u32[]{:S(2)}, u32[]{:S(2)}) async-start(bf16[16,1,2,2048]{3,2,1,0:T(2,128)(2,1)} %bitcast.359), calls=%async_computation.2 | async-start | bytes 262144 | tf_op jit(solution)/shard_map/while/body/eval_jaxpr/all_to_all | solution.py:162
  522.0 12.0 %all-to-all-start.3 = ((bf16[16,1,2,2048]{3,2,1,0:T(2,128)(2,1)}), bf16[16,1,2,2048]{3,2,1,0:T(2,128)(2,1)S(1)}, u32[]{:S(2)}, u32[]{:S(2)}) async-start(bf16[16,1,2,2048]{3,2,1,0:T(2,128)(2,1)} %copy.87), calls=%async_computation.3 | async-start | bytes 262144 | tf_op jit(solution)/shard_map/while/body/eval_jaxpr/all_to_all | solution.py:167
  549.2 12.6 %all-to-all-start.2 = ((bf16[16,1,2,2048]{3,2,1,0:T(2,128)(2,1)}), bf16[16,1,2,2048]{3,2,1,0:T(2,128)(2,1)S(1)}, u32[]{:S(2)}, u32[]{:S(2)}) async-start(bf16[16,1,2,2048]{3,2,1,0:T(2,128)(2,1)} %bitcast.359), calls=%async_computation.2 | async-start | bytes 262144 | tf_op jit(solution)/shard_map/while/body/eval_jaxpr/all_to_all | solution.py:162
  566.9 12.0 %all-to-all-start.3 = ((bf16[16,1,2,2048]{3,2,1,0:T(2,128)(2,1)}), bf16[16,1,2,2048]{3,2,1,0:T(2,128)(2,1)S(1)}, u32[]{:S(2)}, u32[]{:S(2)}) async-start(bf16[16,1,2,2048]{3,2,1,0:T(2,128)(2,1)} %copy.87), calls=%async_computation.3 | async-start | bytes 262144 | tf_op jit(solution)/shard_map/while/body/eval_jaxpr/all_to_all | solution.py:167
  581.7 6.1 collective-permute-start.1
  594.0 12.6 %all-to-all-start.2 = ((bf16[16,1,2,2048]{3,2,1,0:T(2,128)(2,1)}), bf16[16,1,2,2048]{3,2,1,0:T(2,128)(2,1)S(1)}, u32[]{:S(2)}, u32[]{:S(2)}) async-start(bf16[16,1,2,2048]{3,2,1,0:T(2,128)(2,1)} %bitcast.359), calls=%async_computation.2 | async-start | bytes 262144 | tf_op jit(solution)/shard_map/while/body/eval_jaxpr/all_to_all | solution.py:162
  611.7 12.0 %all-to-all-start.3 = ((bf16[16,1,2,2048]{3,2,1,0:T(2,128)(2,1)}), bf16[16,1,2,2048]{3,2,1,0:T(2,128)(2,1)S(1)}, u32[]{:S(2)}, u32[]{:S(2)}) async-start(bf16[16,1,2,2048]{3,2,1,0:T(2,128)(2,1)} %copy.87), calls=%async_computation.3 | async-start | bytes 262144 | tf_op jit(solution)/shard_map/while/body/eval_jaxpr/all_to_all | solution.py:167
  638.9 12.6 %all-to-all-start.2 = ((bf16[16,1,2,2048]{3,2,1,0:T(2,128)(2,1)}), bf16[16,1,2,2048]{3,2,1,0:T(2,128)(2,1)S(1)}, u32[]{:S(2)}, u32[]{:S(2)}) async-start(bf16[16,1,2,2048]{3,2,1,0:T(2,128)(2,1)} %bitcast.359), calls=%async_computation.2 | async-start | bytes 262144 | tf_op jit(solution)/shard_map/while/body/eval_jaxpr/all_to_all | solution.py:162
  656.6 12.0 %all-to-all-start.3 = ((bf16[16,1,2,2048]{3,2,1,0:T(2,128)(2,1)}), bf16[16,1,2,2048]{3,2,1,0:T(2,128)(2,1)S(1)}, u32[]{:S(2)}, u32[]{:S(2)}) async-start(bf16[16,1,2,2048]{3,2,1,0:T(2,128)(2,1)} %copy.87), calls=%async_computation.3 | async-start | bytes 262144 | tf_op jit(solution)/shard_map/while/body/eval_jaxpr/all_to_all | solution.py:167
  683.8 12.6 %all-to-all-start.2 = ((bf16[16,1,2,2048]{3,2,1,0:T(2,128)(2,1)}), bf16[16,1,2,2048]{3,2,1,0:T(2,128)(2,1)S(1)}, u32[]{:S(2)}, u32[]{:S(2)}) async-start(bf16[16,1,2,2048]{3,2,1,0:T(2,128)(2,1)} %bitcast.359), calls=%async_computation.2 | async-start | bytes 262144 | tf_op jit(solution)/shard_map/while/body/eval_jaxpr/all_to_all | solution.py:162
  701.5 12.0 %all-to-all-start.3 = ((bf16[16,1,2,2048]{3,2,1,0:T(2,128)(2,1)}), bf16[16,1,2,2048]{3,2,1,0:T(2,128)(2,1)S(1)}, u32[]{:S(2)}, u32[]{:S(2)}) async-start(bf16[16,1,2,2048]{3,2,1,0:T(2,128)(2,1)} %copy.87), calls=%async_computation.3 | async-start | bytes 262144 | tf_op jit(solution)/shard_map/while/body/eval_jaxpr/all_to_all | solution.py:167
  728.7 12.6 %all-to-all-start.2 = ((bf16[16,1,2,2048]{3,2,1,0:T(2,128)(2,1)}), bf16[16,1,2,2048]{3,2,1,0:T(2,128)(2,1)S(1)}, u32[]{:S(2)}, u32[]{:S(2)}) async-start(bf16[16,1,2,2048]{3,2,1,0:T(2,128)(2,1)} %bitcast.359), calls=%async_computation.2 | async-start | bytes 262144 | tf_op jit(solution)/shard_map/while/body/eval_jaxpr/all_to_all | solution.py:162
  746.4 12.0 %all-to-all-start.3 = ((bf16[16,1,2,2048]{3,2,1,0:T(2,128)(2,1)}), bf16[16,1,2,2048]{3,2,1,0:T(2,128)(2,1)S(1)}, u32[]{:S(2)}, u32[]{:S(2)}) async-start(bf16[16,1,2,2048]{3,2,1,0:T(2,128)(2,1)} %copy.87), calls=%async_computation.3 | async-start | bytes 262144 | tf_op jit(solution)/shard_map/while/body/eval_jaxpr/all_to_all | solution.py:167
  768.0 89.0 %reduce-scatter.2.cloned.1.call-start = ((), (), s32[]{:S(2)}) async-start(), calls=%async_computation.5 | async-start | bytes 786432 | tf_op jit(solution)/shard_map/reduce_scatter | solution.py:227
  (40 other events, 570.7 us)
Sparse Core Ops, SparseCore 0:
  768.1 87.3 all-reduce.1
Sparse Core Ops, SparseCore 1:
  771.3 13.1 reduce-scatter.1
where the time goes:
time: 874 us; the launch traced here: 864 us
  starting transfers between devices  235 us (27%)
  waiting for transfers between devices  194 us (22%)
  matrix products  157 us (18%)
  other arithmetic  119 us (14%)
  local copies, waits for them, and re-layouts  90.7 us (10%)
  blocking collectives  51.6 us (6%)
  between operations  15.6 us (2%)
    dynamic_update_slice x63, other arithmetic, keep_row(): lax.dynamic_update_index_in_dim(stash, jnp.where(active, value, old_row),...  67.9 us
    all_to_all x9, starting transfers between devices, backward_tick(): lax.all_to_all(rows_grad, ('expert', 'dp'), split_axis=0, concat_axis=0,...  54.7 us
    dot_general x18, matrix products, expert_inner(): jnp.einsum('sekd,edf->sekf', exp_rows, w_gu, preferred_element_type=jnp.f...  54.1 us
    ppermute x18, starting transfers between devices, shifted(): lax.ppermute(value, axis, [(source, source + steps) for source in range(l...  49.1 us
    all_to_all x9, waiting for transfers between devices, expert_forward(): lax.all_to_all(out_rows, ('expert', 'dp'), split_axis=0, concat_axis=0, t...  47.7 us
    all_to_all x9, starting transfers between devices, forward_tick(): lax.all_to_all(send_rows, ('expert', 'dp'), split_axis=0, concat_axis=0,...  44.6 us
    psum x1, waiting for transfers between devices, local(): lax.psum(acc_router.astype(jnp.bfloat16), ('expert', 'dp'))  43.3 us
    all_to_all x9, starting transfers between devices, backward_tick(): lax.all_to_all(dy_send, ('expert', 'dp'), split_axis=0, concat_axis=0, ti...  43.3 us
  transfers between devices with their start and end apart: 56, of which 46 were waited for; matrix products, arithmetic and copies ran while one was open for 18% of the time, Pallas kernels for 0%

commit v1 on v0

--- a/solution.py
+++ b/solution.py
@@ -4,6 +4,29 @@
 from jax.sharding import PartitionSpec as P
 
 EPS = 1e-05
+
+
+def cut_along(value, dim, length):
+    dims = value.shape
+    blocks = value.reshape(*dims[:dim], length, dims[dim] // length, *dims[dim + 1 :])
+    return jnp.moveaxis(blocks, dim, 0)
+
+
+def in_order(tiles, dim):
+    tiles = jnp.moveaxis(tiles, 0, dim)
+    lengths = tiles.shape
+    return tiles.reshape(*lengths[:dim], lengths[dim] * lengths[dim + 1], *lengths[dim + 2 :])
+
+
+def sent_to_each(array, axis, split_dim, concat_dim):
+    count, index = (lax.axis_size(axis), lax.axis_index(axis))
+    blocks = cut_along(array, split_dim, count)
+    done = [blocks[index]]
+    for turn in range(1, count):
+        sent = blocks[(index + turn) % count]
+        done.append(lax.ppermute(sent, axis, [(i, (i + turn) % count) for i in range(count)]))
+    blocks = jnp.stack(done)[(index - jnp.arange(count)) % count]
+    return in_order(blocks, concat_dim)
 
 
 def shifted(value, axis, steps):
@@ -114,9 +137,7 @@
         expert_hits, slot_place = slot_tables(route_rows, n_expert, capacity)
         send_rows = jnp.einsum("ktc,td->cd", slot_place, normed, preferred_element_type=jnp.float32)
         send_rows = send_rows.astype(jnp.bfloat16).reshape(rows_shape)
-        returned, landed = expert_forward(
-            lax.all_to_all(send_rows, ("expert", "dp"), split_axis=0, concat_axis=0, tiled=True)
-        )
+        returned, landed = expert_forward(sent_to_each(send_rows, ("expert", "dp"), 0, 0))
         back_flat = returned.reshape(cells, model_width)
         picked = jnp.einsum(
             "ktc,cd->ktd", slot_place, back_flat, preferred_element_type=jnp.float32

time: 874 us -> 1020 us (1.17)
  starting transfers between devices: 235 us -> 386 us
  waiting for transfers between devices: 194 us -> 182 us
    ppermute x0 -> x135, starting transfers between devices: none -> 184 us  [sent_to_each(): lax.ppermute(sent, axis, [(i, (i + turn) % count) for i in range(count)])]
    all_to_all x9 -> x0, starting transfers between devices: 44.6 us -> none  [forward_tick(): lax.all_to_all(send_rows, ('expert', 'dp'), split_axis=0, concat_axis=0,...]
    all_to_all x9 -> x0, waiting for transfers between devices: 34.5 us -> none  [forward_tick(): lax.all_to_all(send_rows, ('expert', 'dp'), split_axis=0, concat_axis=0,...]
    ppermute x0 -> x135, waiting for transfers between devices: none -> 31.9 us  [sent_to_each(): lax.ppermute(sent, axis, [(i, (i + turn) % count) for i in range(count)])]
    all_to_all x9, starting transfers between devices: 43.1 us -> 54.6 us  [expert_forward(): lax.all_to_all(out_rows, ('expert', 'dp'), split_axis=0, concat_axis=0, t...]
    dynamic_slice x45 -> x36, local copies, waits for them, and re-layouts: 32.7 us -> 23.6 us  [keep_row(): old_row = lax.dynamic_index_in_dim(stash, position, 0, keepdims=False)]
  transfers between devices with their start and end apart: 56 -> 182, of which waited for: 46 -> 55; matrix products, arithmetic and copies ran while one was open for 18% -> 16% of each run, Pallas kernels for 0% -> 0%
where the time goes in v1:
time: 1020 us; the launch traced here: 1010 us
  starting transfers between devices  386 us (38%)
  waiting for transfers between devices  182 us (18%)
  matrix products  157 us (15%)
  other arithmetic  128 us (13%)
  local copies, waits for them, and re-layouts  86.4 us (8%)
  blocking collectives  51.6 us (5%)
  between operations  15.6 us (2%)
    ppermute x135, starting transfers between devices, sent_to_each(): lax.ppermute(sent, axis, [(i, (i + turn) % count) for i in range(count)])  184 us
    dynamic_update_slice x63, other arithmetic, keep_row(): lax.dynamic_update_index_in_dim(stash, jnp.where(active, value, old_row),...  76 us
    all_to_all x9, starting transfers between devices, backward_tick(): lax.all_to_all(rows_grad, ('expert', 'dp'), split_axis=0, concat_axis=0,...  54.7 us
    all_to_all x9, starting transfers between devices, expert_forward(): lax.all_to_all(out_rows, ('expert', 'dp'), split_axis=0, concat_axis=0, t...  54.6 us
    dot_general x18, matrix products, expert_inner(): jnp.einsum('sekd,edf->sekf', exp_rows, w_gu, preferred_element_type=jnp.f...  54.2 us
    ppermute x18, starting transfers between devices, shifted(): lax.ppermute(value, axis, [(source, source + steps) for source in range(l...  49 us
    all_to_all x9, starting transfers between devices, backward_tick(): lax.all_to_all(dy_send, ('expert', 'dp'), split_axis=0, concat_axis=0, ti...  43.3 us
    psum x1, waiting for transfers between devices, local(): lax.psum(acc_router.astype(jnp.bfloat16), ('expert', 'dp'))  43.2 us
  transfers between devices with their start and end apart: 182, of which 55 were waited for; matrix products, arithmetic and copies ran while one was open for 16% of the time, Pallas kernels for 0%

profile of v1, /device:TPU:8, one launch (start us, length us, event | category | flops | bytes accessed | tf_op | source)
XLA Modules:
  0.0 1009.6 jit_solution(9972396503070231381)
XLA Ops:
  8.1 10.6 %all_gather.6 = bf16[8,16,2048]{2,1,0:T(8,128)(2,1)} all-gather(bf16[8,16,1024]{2,1,0:T(8,128)(2,1)} %param.12), channel_id=1, replica_groups=mesh['section'=2,'expert'=4,'dp'=4] {'section'}, dimensions={2}, use_global_device_ids=true | all-gather | bytes 786432 | tf_op jit(solution)/shard_map/all_gather | solution.py:108
  18.6 8.9 all_gather.7
  31.9 472.6 %while.49 = (s32[]{:T(128)}, bf16[16,2048]{1,0:T(8,128)(2,1)S(1)}, bf16[8,16,2048]{2,1,0:T(8,128)(2,1)S(1)}, bf16[8,32,2048]{2,1,0:T(8,128)(2,1)}, bf16[8,16,1,2...) while((s32[]{:T(128)}, bf16[16,2048]{1,0:T(8,128)(2,1)S(1)}, ...), condition=%wide.region_7.8_spmd, body=%wide.region_0.7_spmd.sunk | while | flops 209599856 | bytes 12243797 | solution.py:161
  66.9 4.9 all-to-all-start
  73.5 4.3 all-to-all-done
  117.4 6.2 all-to-all-start
  125.3 4.3 all-to-all-done
  129.9 4.3 collective-permute-start.15
  170.0 6.2 all-to-all-start
  182.6 4.3 collective-permute-start.15
  222.6 6.2 all-to-all-start
  230.5 4.3 all-to-all-done
  235.2 4.3 collective-permute-start.15
  275.3 6.2 all-to-all-start
  283.2 4.3 all-to-all-done
  287.8 4.3 collective-permute-start.15
  327.9 6.2 all-to-all-start
  335.8 4.3 all-to-all-done
  340.5 4.3 collective-permute-start.15
  380.5 6.2 all-to-all-start
  388.4 4.3 all-to-all-done
  393.1 4.3 collective-permute-start.15
  433.2 6.2 all-to-all-start
  445.7 4.3 collective-permute-start.15
  485.8 6.2 all-to-all-start
  498.3 4.3 collective-permute-start.15
  508.6 403.9 %while.50 = (s32[]{:T(128)}, bf16[16,2048]{1,0:T(8,128)(2,1)S(1)}, bf16[8,16,1,2,2048]{4,3,1,2,0:T(2,128)(2,1)}, bf16[8,16,1,2,512]{4,1,3,2,0:T(8,128)(2,1)}, bf...) while((s32[]{:T(128)}, bf16[16,2048]{1,0:T(8,128)(2,1)S(1)}, ...), condition=%wide.region_18.19_spmd.clone, body=%wide.region_8.18_spmd.clone.sunk | while | flops 361911744 | bytes 17806364 | solution.py:235
  514.9 4.8 all-to-all-start.1
  532.6 6.1 all-to-all-start.2
  559.7 4.8 all-to-all-start.1
  577.4 6.1 all-to-all-start.2
  604.6 4.8 all-to-all-start.1
  622.3 6.1 all-to-all-start.2
  649.5 4.8 all-to-all-start.1
  667.2 6.1 all-to-all-start.2
  694.4 4.8 all-to-all-start.1
  712.1 6.1 all-to-all-start.2
  739.2 4.8 all-to-all-start.1
  756.9 6.1 all-to-all-start.2
  784.1 4.8 all-to-all-start.1
  801.8 6.1 all-to-all-start.2
  829.0 4.8 all-to-all-start.1
  846.7 6.1 all-to-all-start.2
  873.9 4.8 all-to-all-start.1
  891.6 6.1 all-to-all-start.2
  915.5 6.2 convolution_bitcast_fusion.1
  921.7 32.1 %psum.15 = bf16[1,2048]{1,0:T(2,128)(2,1)S(1)} all-reduce(bf16[1,2048]{1,0:T(2,128)(2,1)S(1)} %broadcast_in_dim.182), channel_id=1, replica_groups=mesh['section'=2,'expert'=4,'dp'=4] {'expert','dp'}, use_global_device_ids=true, to_apply=%region_21.22 | all-reduce | flops 2048 | bytes 8192 | tf_op jit(solution)/shard_map/psum | solution.py:245
  957.5 43.2 %all-reduce.2.cloned.1.call-done = bf16[1,2048,16]{1,2,0:T(8,128)(2,1)} async-done(((bf16[1,2048,16]{1,2,0:T(8,128)(2,1)}), bf16[1,2048,16]{1,2,0:T(8,128)(2,1)}) %all-reduce.2.cloned.1.call-update) | async-done | bytes 65552 | tf_op jit(solution)/shard_map/psum | solution.py:244
  (1127 shorter events, 676.7 us)
Async XLA Ops:
  8.0 992.7 %all-reduce.2.cloned.1.call-start = ((), (), s32[]{:S(2)}) async-start(), calls=%async_computation.5 | async-start | bytes 131072 | tf_op jit(solution)/shard_map/psum | solution.py:244
  38.0 8.8 collective-permute-start.3
  41.0 8.8 collective-permute-start.4
  42.3 9.7 collective-permute-start.5
  66.9 10.9 %all-to-all-start = ((bf16[16,1,2,2048]{3,2,1,0:T(2,128)(2,1)}), bf16[16,1,2,2048]{3,2,1,0:T(2,128)(2,1)S(1)}, u32[]{:S(2)}, u32[]{:S(2)}) async-start(bf16[16,1,2,2048]{3,2,1,0:T(2,128)(2,1)} %copy.81), calls=%async_computation | async-start | bytes 262144 | tf_op jit(solution)/shard_map/while/body/eval_jaxpr/all_to_all | solution.py:124
  90.9 9.1 collective-permute-start.4
  94.7 9.3 collective-permute-start.5
  117.4 12.2 %all-to-all-start = ((bf16[16,1,2,2048]{3,2,1,0:T(2,128)(2,1)}), bf16[16,1,2,2048]{3,2,1,0:T(2,128)(2,1)S(1)}, u32[]{:S(2)}, u32[]{:S(2)}) async-start(bf16[16,1,2,2048]{3,2,1,0:T(2,128)(2,1)} %copy.81), calls=%async_computation | async-start | bytes 262144 | tf_op jit(solution)/shard_map/while/body/eval_jaxpr/all_to_all | solution.py:124
  143.6 9.1 collective-permute-start.4
  147.3 9.3 collective-permute-start.5
  170.0 12.2 %all-to-all-start = ((bf16[16,1,2,2048]{3,2,1,0:T(2,128)(2,1)}), bf16[16,1,2,2048]{3,2,1,0:T(2,128)(2,1)S(1)}, u32[]{:S(2)}, u32[]{:S(2)}) async-start(bf16[16,1,2,2048]{3,2,1,0:T(2,128)(2,1)} %copy.81), calls=%async_computation | async-start | bytes 262144 | tf_op jit(solution)/shard_map/while/body/eval_jaxpr/all_to_all | solution.py:124
  196.2 9.1 collective-permute-start.4
  199.9 9.3 collective-permute-start.5
  222.6 12.2 %all-to-all-start = ((bf16[16,1,2,2048]{3,2,1,0:T(2,128)(2,1)}), bf16[16,1,2,2048]{3,2,1,0:T(2,128)(2,1)S(1)}, u32[]{:S(2)}, u32[]{:S(2)}) async-start(bf16[16,1,2,2048]{3,2,1,0:T(2,128)(2,1)} %copy.81), calls=%async_computation | async-start | bytes 262144 | tf_op jit(solution)/shard_map/while/body/eval_jaxpr/all_to_all | solution.py:124
  248.8 9.1 collective-permute-start.4
  252.6 9.3 collective-permute-start.5
  275.3 12.2 %all-to-all-start = ((bf16[16,1,2,2048]{3,2,1,0:T(2,128)(2,1)}), bf16[16,1,2,2048]{3,2,1,0:T(2,128)(2,1)S(1)}, u32[]{:S(2)}, u32[]{:S(2)}) async-start(bf16[16,1,2,2048]{3,2,1,0:T(2,128)(2,1)} %copy.81), calls=%async_computation | async-start | bytes 262144 | tf_op jit(solution)/shard_map/while/body/eval_jaxpr/all_to_all | solution.py:124
  301.5 9.1 collective-permute-start.4
  305.2 9.3 collective-permute-start.5
  327.9 12.2 %all-to-all-start = ((bf16[16,1,2,2048]{3,2,1,0:T(2,128)(2,1)}), bf16[16,1,2,2048]{3,2,1,0:T(2,128)(2,1)S(1)}, u32[]{:S(2)}, u32[]{:S(2)}) async-start(bf16[16,1,2,2048]{3,2,1,0:T(2,128)(2,1)} %copy.81), calls=%async_computation | async-start | bytes 262144 | tf_op jit(solution)/shard_map/while/body/eval_jaxpr/all_to_all | solution.py:124
  354.1 9.1 collective-permute-start.4
  357.8 9.3 collective-permute-start.5
  380.5 12.2 %all-to-all-start = ((bf16[16,1,2,2048]{3,2,1,0:T(2,128)(2,1)}), bf16[16,1,2,2048]{3,2,1,0:T(2,128)(2,1)S(1)}, u32[]{:S(2)}, u32[]{:S(2)}) async-start(bf16[16,1,2,2048]{3,2,1,0:T(2,128)(2,1)} %copy.81), calls=%async_computation | async-start | bytes 262144 | tf_op jit(solution)/shard_map/while/body/eval_jaxpr/all_to_all | solution.py:124
  406.7 9.1 collective-permute-start.4
  410.5 9.3 collective-permute-start.5
  433.2 12.2 %all-to-all-start = ((bf16[16,1,2,2048]{3,2,1,0:T(2,128)(2,1)}), bf16[16,1,2,2048]{3,2,1,0:T(2,128)(2,1)S(1)}, u32[]{:S(2)}, u32[]{:S(2)}) async-start(bf16[16,1,2,2048]{3,2,1,0:T(2,128)(2,1)} %copy.81), calls=%async_computation | async-start | bytes 262144 | tf_op jit(solution)/shard_map/while/body/eval_jaxpr/all_to_all | solution.py:124
  459.4 9.1 collective-permute-start.4
  463.1 9.3 collective-permute-start.5
  485.8 12.2 %all-to-all-start = ((bf16[16,1,2,2048]{3,2,1,0:T(2,128)(2,1)}), bf16[16,1,2,2048]{3,2,1,0:T(2,128)(2,1)S(1)}, u32[]{:S(2)}, u32[]{:S(2)}) async-start(bf16[16,1,2,2048]{3,2,1,0:T(2,128)(2,1)} %copy.81), calls=%async_computation | async-start | bytes 262144 | tf_op jit(solution)/shard_map/while/body/eval_jaxpr/all_to_all | solution.py:124
  514.9 12.6 %all-to-all-start.1 = ((bf16[16,1,2,2048]{3,2,1,0:T(2,128)(2,1)}), bf16[16,1,2,2048]{3,2,1,0:T(2,128)(2,1)S(1)}, u32[]{:S(2)}, u32[]{:S(2)}) async-start(bf16[16,1,2,2048]{3,2,1,0:T(2,128)(2,1)} %bitcast.444), calls=%async_computation.1 | async-start | bytes 262144 | tf_op jit(solution)/shard_map/while/body/eval_jaxpr/all_to_all | solution.py:183
  532.6 12.0 %all-to-all-start.2 = ((bf16[16,1,2,2048]{3,2,1,0:T(2,128)(2,1)}), bf16[16,1,2,2048]{3,2,1,0:T(2,128)(2,1)S(1)}, u32[]{:S(2)}, u32[]{:S(2)}) async-start(bf16[16,1,2,2048]{3,2,1,0:T(2,128)(2,1)} %copy.84), calls=%async_computation.2 | async-start | bytes 262144 | tf_op jit(solution)/shard_map/while/body/eval_jaxpr/all_to_all | solution.py:188
  559.7 12.6 %all-to-all-start.1 = ((bf16[16,1,2,2048]{3,2,1,0:T(2,128)(2,1)}), bf16[16,1,2,2048]{3,2,1,0:T(2,128)(2,1)S(1)}, u32[]{:S(2)}, u32[]{:S(2)}) async-start(bf16[16,1,2,2048]{3,2,1,0:T(2,128)(2,1)} %bitcast.444), calls=%async_computation.1 | async-start | bytes 262144 | tf_op jit(solution)/shard_map/while/body/eval_jaxpr/all_to_all | solution.py:183
  577.4 12.0 %all-to-all-start.2 = ((bf16[16,1,2,2048]{3,2,1,0:T(2,128)(2,1)}), bf16[16,1,2,2048]{3,2,1,0:T(2,128)(2,1)S(1)}, u32[]{:S(2)}, u32[]{:S(2)}) async-start(bf16[16,1,2,2048]{3,2,1,0:T(2,128)(2,1)} %copy.84), calls=%async_computation.2 | async-start | bytes 262144 | tf_op jit(solution)/shard_map/while/body/eval_jaxpr/all_to_all | solution.py:188
  604.6 12.6 %all-to-all-start.1 = ((bf16[16,1,2,2048]{3,2,1,0:T(2,128)(2,1)}), bf16[16,1,2,2048]{3,2,1,0:T(2,128)(2,1)S(1)}, u32[]{:S(2)}, u32[]{:S(2)}) async-start(bf16[16,1,2,2048]{3,2,1,0:T(2,128)(2,1)} %bitcast.444), calls=%async_computation.1 | async-start | bytes 262144 | tf_op jit(solution)/shard_map/while/body/eval_jaxpr/all_to_all | solution.py:183
  622.3 12.0 %all-to-all-start.2 = ((bf16[16,1,2,2048]{3,2,1,0:T(2,128)(2,1)}), bf16[16,1,2,2048]{3,2,1,0:T(2,128)(2,1)S(1)}, u32[]{:S(2)}, u32[]{:S(2)}) async-start(bf16[16,1,2,2048]{3,2,1,0:T(2,128)(2,1)} %copy.84), calls=%async_computation.2 | async-start | bytes 262144 | tf_op jit(solution)/shard_map/while/body/eval_jaxpr/all_to_all | solution.py:188
  649.5 12.6 %all-to-all-start.1 = ((bf16[16,1,2,2048]{3,2,1,0:T(2,128)(2,1)}), bf16[16,1,2,2048]{3,2,1,0:T(2,128)(2,1)S(1)}, u32[]{:S(2)}, u32[]{:S(2)}) async-start(bf16[16,1,2,2048]{3,2,1,0:T(2,128)(2,1)} %bitcast.444), calls=%async_computation.1 | async-start | bytes 262144 | tf_op jit(solution)/shard_map/while/body/eval_jaxpr/all_to_all | solution.py:183
  667.2 12.0 %all-to-all-start.2 = ((bf16[16,1,2,2048]{3,2,1,0:T(2,128)(2,1)}), bf16[16,1,2,2048]{3,2,1,0:T(2,128)(2,1)S(1)}, u32[]{:S(2)}, u32[]{:S(2)}) async-start(bf16[16,1,2,2048]{3,2,1,0:T(2,128)(2,1)} %copy.84), calls=%async_computation.2 | async-start | bytes 262144 | tf_op jit(solution)/shard_map/while/body/eval_jaxpr/all_to_all | solution.py:188
  694.4 12.6 %all-to-all-start.1 = ((bf16[16,1,2,2048]{3,2,1,0:T(2,128)(2,1)}), bf16[16,1,2,2048]{3,2,1,0:T(2,128)(2,1)S(1)}, u32[]{:S(2)}, u32[]{:S(2)}) async-start(bf16[16,1,2,2048]{3,2,1,0:T(2,128)(2,1)} %bitcast.444), calls=%async_computation.1 | async-start | bytes 262144 | tf_op jit(solution)/shard_map/while/body/eval_jaxpr/all_to_all | solution.py:183
  712.1 12.0 %all-to-all-start.2 = ((bf16[16,1,2,2048]{3,2,1,0:T(2,128)(2,1)}), bf16[16,1,2,2048]{3,2,1,0:T(2,128)(2,1)S(1)}, u32[]{:S(2)}, u32[]{:S(2)}) async-start(bf16[16,1,2,2048]{3,2,1,0:T(2,128)(2,1)} %copy.84), calls=%async_computation.2 | async-start | bytes 262144 | tf_op jit(solution)/shard_map/while/body/eval_jaxpr/all_to_all | solution.py:188
  739.2 12.6 %all-to-all-start.1 = ((bf16[16,1,2,2048]{3,2,1,0:T(2,128)(2,1)}), bf16[16,1,2,2048]{3,2,1,0:T(2,128)(2,1)S(1)}, u32[]{:S(2)}, u32[]{:S(2)}) async-start(bf16[16,1,2,2048]{3,2,1,0:T(2,128)(2,1)} %bitcast.444), calls=%async_computation.1 | async-start | bytes 262144 | tf_op jit(solution)/shard_map/while/body/eval_jaxpr/all_to_all | solution.py:183
  756.9 12.0 %all-to-all-start.2 = ((bf16[16,1,2,2048]{3,2,1,0:T(2,128)(2,1)}), bf16[16,1,2,2048]{3,2,1,0:T(2,128)(2,1)S(1)}, u32[]{:S(2)}, u32[]{:S(2)}) async-start(bf16[16,1,2,2048]{3,2,1,0:T(2,128)(2,1)} %copy.84), calls=%async_computation.2 | async-start | bytes 262144 | tf_op jit(solution)/shard_map/while/body/eval_jaxpr/all_to_all | solution.py:188
  784.1 12.6 %all-to-all-start.1 = ((bf16[16,1,2,2048]{3,2,1,0:T(2,128)(2,1)}), bf16[16,1,2,2048]{3,2,1,0:T(2,128)(2,1)S(1)}, u32[]{:S(2)}, u32[]{:S(2)}) async-start(bf16[16,1,2,2048]{3,2,1,0:T(2,128)(2,1)} %bitcast.444), calls=%async_computation.1 | async-start | bytes 262144 | tf_op jit(solution)/shard_map/while/body/eval_jaxpr/all_to_all | solution.py:183
  801.8 12.0 %all-to-all-start.2 = ((bf16[16,1,2,2048]{3,2,1,0:T(2,128)(2,1)}), bf16[16,1,2,2048]{3,2,1,0:T(2,128)(2,1)S(1)}, u32[]{:S(2)}, u32[]{:S(2)}) async-start(bf16[16,1,2,2048]{3,2,1,0:T(2,128)(2,1)} %copy.84), calls=%async_computation.2 | async-start | bytes 262144 | tf_op jit(solution)/shard_map/while/body/eval_jaxpr/all_to_all | solution.py:188
  829.0 12.6 %all-to-all-start.1 = ((bf16[16,1,2,2048]{3,2,1,0:T(2,128)(2,1)}), bf16[16,1,2,2048]{3,2,1,0:T(2,128)(2,1)S(1)}, u32[]{:S(2)}, u32[]{:S(2)}) async-start(bf16[16,1,2,2048]{3,2,1,0:T(2,128)(2,1)} %bitcast.444), calls=%async_computation.1 | async-start | bytes 262144 | tf_op jit(solution)/shard_map/while/body/eval_jaxpr/all_to_all | solution.py:183
  846.7 12.0 %all-to-all-start.2 = ((bf16[16,1,2,2048]{3,2,1,0:T(2,128)(2,1)}), bf16[16,1,2,2048]{3,2,1,0:T(2,128)(2,1)S(1)}, u32[]{:S(2)}, u32[]{:S(2)}) async-start(bf16[16,1,2,2048]{3,2,1,0:T(2,128)(2,1)} %copy.84), calls=%async_computation.2 | async-start | bytes 262144 | tf_op jit(solution)/shard_map/while/body/eval_jaxpr/all_to_all | solution.py:188
  873.9 12.6 %all-to-all-start.1 = ((bf16[16,1,2,2048]{3,2,1,0:T(2,128)(2,1)}), bf16[16,1,2,2048]{3,2,1,0:T(2,128)(2,1)S(1)}, u32[]{:S(2)}, u32[]{:S(2)}) async-start(bf16[16,1,2,2048]{3,2,1,0:T(2,128)(2,1)} %bitcast.444), calls=%async_computation.1 | async-start | bytes 262144 | tf_op jit(solution)/shard_map/while/body/eval_jaxpr/all_to_all | solution.py:183
  891.6 12.0 %all-to-all-start.2 = ((bf16[16,1,2,2048]{3,2,1,0:T(2,128)(2,1)}), bf16[16,1,2,2048]{3,2,1,0:T(2,128)(2,1)S(1)}, u32[]{:S(2)}, u32[]{:S(2)}) async-start(bf16[16,1,2,2048]{3,2,1,0:T(2,128)(2,1)} %copy.84), calls=%async_computation.2 | async-start | bytes 262144 | tf_op jit(solution)/shard_map/while/body/eval_jaxpr/all_to_all | solution.py:188
  913.2 89.0 %reduce-scatter.2.cloned.1.call-start = ((), (), s32[]{:S(2)}) async-start(), calls=%async_computation.4 | async-start | bytes 786432 | tf_op jit(solution)/shard_map/reduce_scatter | solution.py:248
  (166 other events, 1396.7 us)
Sparse Core Ops, SparseCore 0:
  913.3 87.3 all-reduce.1
Sparse Core Ops, SparseCore 1:
  916.5 13.1 reduce-scatter.1
